TPU v7x, 32 devices: a whole 2x2x4 slice. The times are simulated.
32 devices in a mesh: wav: 8 (over y, x, core), lev: 4 (over z).
Axes of the slice: x: 2, y: 2, z: 4, core: 2. Of those that a mesh axis runs over, the one named last changes fastest.
Arguments:
- spectral: bfloat16 [200, 401, 512], P('wav', None, 'lev'), may hold values from -0.1796875 to 0.1796875
- legendre: bfloat16 [200, 401, 64], P('wav', None, 'lev'), may hold values from -0.4375 to 0.4375
- wave_pair: int32 [200], replicated, may hold values from -1 to 199, as said below
- lat_slot: int32 [64], replicated, may hold values from 0 to 799, as said below
Outputs:
- gridded: bfloat16 [64, 256, 1616], P('wav', 'lev')
Inputs may be any that keep to these rules, and one draw needn't show every extreme that they name: `wave_pair`: each pair number 0 to 199 appears exactly once; all other entries are -1. `lat_slot`: the entries are distinct latitudes.
All inputs are finite; a program needn't handle non-finite values.
Results may differ from a plain program's by a relative error of at most 0.0055.
Values may be sent and summed in bfloat16 or wider, within the bound.
A program may use at most 64 MiB of HBM per device.

v0:
```python
import functools
import math

import jax
import jax.numpy as jnp
from jax import lax
from jax.experimental import pallas as pl
from jax.experimental.pallas import tpu as pltpu
from jax.sharding import PartitionSpec as P

NLAT = 800
CH = 16
LANE = 128
KB = 64


def half_turn(x):
    u = x * math.pi
    v = u * u
    s = -2.5052108385441720e-08
    for coef in (2.7557319223985893e-06, -1.9841269841269841e-04, 8.3333333333333333e-03, -1.6666666666666667e-01, 1.0):
        s = s * v + coef
    s = s * u
    c = -2.7557319223985888e-07
    for coef in (2.4801587301587302e-05, -1.3888888888888889e-03, 4.1666666666666667e-02, -0.5, 1.0):
        c = c * v + coef
    return 1.0 - 2.0 * s * s, 2.0 * s * c


def trig(prod, count, inv):
    r = prod - jnp.floor(prod * inv + 0.5) * count
    return half_turn(r * inv)


def kernel(
    nw, nl, slots, wave_count, half_width,
    wp_ref, lat_ref, spec_ref, leg_ref, out_ref,
    spec, own, leg, tail, expand, meven, amp, full, part, stage, snd, rcv, basis, obuf,
    loc_sem, ag_send, ag_recv, aa_send, aa_recv, own_sem, out_sem,
):
    wi = lax.axis_index("wav")
    li = lax.axis_index("lev")
    chunks = snd.shape[0]
    rows = obuf.shape[0]
    fold = spec.shape[1]
    main = leg.shape[3]
    rest = fold - main
    per_tile = LANE // rest
    span = (CH // per_tile) * per_tile
    layers = obuf.shape[1]
    items = 2 * layers
    width = out_ref.shape[2]
    kdim = chunks * nw * CH
    blocks = half_width // LANE
    qtot = nw * rows
    fmt = pl.DeviceIdType.MESH
    bounds = [(c * span, min(slots, (c + 1) * span)) for c in range(chunks)]

    own_copy = pltpu.make_async_copy(leg_ref, own, loc_sem.at[0])
    own_copy.start()
    leg_copy = pltpu.make_async_copy(leg_ref.at[:, :, pl.ds(0, main)], leg.at[li], loc_sem.at[1])
    leg_copy.start()
    spec_copy = pltpu.make_async_copy(spec_ref, spec, loc_sem.at[2])
    spec_copy.start()

    barrier = pltpu.get_barrier_semaphore()
    for d in range(1, nl):
        pl.semaphore_signal(barrier, inc=1, device_id=(wi, lax.rem(li + d, nl)), device_id_type=fmt)
    for d in range(1, nw):
        pl.semaphore_signal(barrier, inc=1, device_id=(lax.rem(wi + d, nw), li), device_id_type=fmt)
    pl.semaphore_wait(barrier, nl - 1 + nw - 1)

    def hop(way, k, c, piece, block):
        lo, hi = bounds[c]
        if piece == 0:
            view = leg.at[block, pl.ds(lo, hi - lo)]
            src = leg_ref.at[pl.ds(lo, hi - lo), :, pl.ds(0, main)] if k == 0 else view
        else:
            view = tail.at[block, c]
            src = view
        return pltpu.make_async_remote_copy(
            src_ref=src,
            dst_ref=view,
            send_sem=ag_send.at[way, k, c, piece],
            recv_sem=ag_recv.at[way, k, c, piece],
            device_id=(wi, li + 1 - 2 * way),
            device_id_type=fmt,
        )

    def sends(way, k):
        if way == 0:
            return (li - k >= 0) & (li + 1 < nl), jnp.maximum(li - k, 0)
        return (li + k < nl) & (li >= 1), jnp.minimum(li + k, nl - 1)

    def receives(way, k):
        if way == 0:
            return li - 1 - k >= 0, jnp.maximum(li - 1 - k, 0)
        return li + 1 + k < nl, jnp.minimum(li + 1 + k, nl - 1)

    def send(k, c, piece):
        for way in range(2):
            going, block = sends(way, k)

            @pl.when(going)
            def _():
                hop(way, k, c, piece, block).start()

    def arrive(k, c):
        for way in range(2):
            coming, block = receives(way, k)

            @pl.when(coming)
            def _():
                hop(way, k, c, 0, block).wait_recv()
                hop(way, k, c, 1, block).wait_recv()

        if k + 1 < nl - 1:
            send(k + 1, c, 0)
            send(k + 1, c, 1)

    def aa(c, d):
        dest = lax.rem(wi + d, nw)
        return pltpu.make_async_remote_copy(
            src_ref=snd.at[c, dest],
            dst_ref=rcv.at[c, wi],
            send_sem=aa_send.at[c, d],
            recv_sem=aa_recv.at[c, d],
            device_id=(dest, li),
            device_id_type=fmt,
        )

    for c in range(chunks):
        send(0, c, 0)
    own_copy.wait()
    place_t = lax.broadcasted_iota(jnp.int32, (rest, LANE), 0)
    place_x = lax.broadcasted_iota(jnp.int32, (rest, LANE), 1)
    for c in range(chunks):
        lo, hi = bounds[c]
        for g in range(tail.shape[2]):
            total = jnp.zeros(tail.shape[3:], jnp.float32)
            for n in range(per_tile):
                s = lo + g * per_tile + n
                if s < hi:
                    place = jnp.where(place_x == place_t + n * rest, 1.0, 0.0).astype(jnp.bfloat16)
                    total += jnp.dot(own[s, :, main:], place, preferred_element_type=jnp.float32)
            tail[li, c, g] = total.astype(jnp.bfloat16)
        send(0, c, 1)

    meven[...] = jnp.full_like(meven, -1.0)

    def place_pairs(src, carry):
        for c in range(chunks):
            lo, hi = bounds[c]
            for s in range(lo, hi):
                p = wp_ref[src * slots + s]
                even = jnp.where(jnp.bitwise_and(p, 1) == 0, p, wave_count - 1 - p)
                even = jnp.where(p < 0, -1, even).astype(jnp.float32)
                meven[pl.ds((c * nw + src) * CH + s - lo, 1), :] = jnp.full((1, LANE), even, jnp.float32)
        return carry

    lax.fori_loop(0, nw, place_pairs, 0)
    out_i = lax.broadcasted_iota(jnp.int32, (items, items), 1)
    in_i = lax.broadcasted_iota(jnp.int32, (items, items), 0)
    perm = jnp.where(
        in_i == jnp.where(out_i < layers, 2 * out_i, 2 * (out_i - layers) + 1), 1.0, 0.0
    ).astype(jnp.bfloat16)

    fine = lax.broadcasted_iota(jnp.int32, (KB, LANE), 1).astype(jnp.float32)
    ahead = lax.broadcasted_iota(jnp.int32, (8, half_width), 1).astype(jnp.float32)
    kchunk = nw * CH
    pieces = kdim // KB

    def turn(x, y):
        return x[0] * y[0] - x[1] * y[1], x[0] * y[1] + x[1] * y[0]

    def minus(pair):
        return pair[0], -pair[1]

    def row_count(r):
        lat = lat_ref[wi * rows + r]
        return 20 + 4 * jnp.minimum(lat, NLAT - 1 - lat)

    def make_basis(step, carry):
        r = lax.div(step, pieces)
        k0 = pl.multiple_of(lax.rem(step, pieces) * KB, KB)
        slab = lax.div(k0, kchunk)
        real = pl.multiple_of(k0 + slab * kchunk, KB)
        imag = pl.multiple_of(real + kchunk, KB)
        count_i = row_count(r)
        highest = jnp.minimum(wave_count - 1, lax.shift_right_logical(count_i - 1, 1)).astype(jnp.float32)
        count = jnp.full((KB, LANE), count_i.astype(jnp.float32), jnp.float32)
        inv = 1.0 / count
        m_even = meven[pl.ds(k0, KB), :]
        for par in range(2):
            m = m_even if par == 0 else (wave_count - 1.0) - m_even
            factor = jnp.where((m >= 0.0) & (m <= highest), jnp.where(m == 0.0, 1.0, 2.0), 0.0)
            amp[r, par, pl.ds(k0, KB), :] = factor.astype(jnp.bfloat16)
        now = minus(trig(m_even * fine, count, inv))
        stride = minus(trig(m_even * LANE, count, inv))
        for b in range(blocks):
            cols = slice(b * LANE, (b + 1) * LANE)
            if b:
                now = turn(now, stride)
            c4 = jnp.broadcast_to(full[r, 0, 0:1, cols], (KB, LANE))
            s4 = jnp.broadcast_to(full[r, 1, 0:1, cols], (KB, LANE))
            basis[r, 0, pl.ds(real, KB), cols] = now[0].astype(jnp.bfloat16)
            basis[r, 0, pl.ds(imag, KB), cols] = now[1].astype(jnp.bfloat16)
            other = (c4 * now[0] + s4 * now[1], s4 * now[0] - c4 * now[1])
            basis[r, 1, pl.ds(real, KB), cols] = other[0].astype(jnp.bfloat16)
            basis[r, 1, pl.ds(imag, KB), cols] = other[1].astype(jnp.bfloat16)
        return carry

    def make_full(r, carry):
        count = jnp.full((8, half_width), row_count(r).astype(jnp.float32), jnp.float32)
        cos_full, neg_sin_full = minus(trig((wave_count - 1.0) * ahead, count, 1.0 / count))
        full[r, 0] = cos_full
        full[r, 1] = neg_sin_full
        return carry

    lax.fori_loop(0, rows, make_full, 0)

    def basis_rows(lo, hi):
        lax.fori_loop(lo * pieces, hi * pieces, make_basis, 0)

    stage[...] = jnp.zeros_like(stage)
    cols = lax.broadcasted_iota(jnp.int32, (1, main), 1)
    tcols = lax.broadcasted_iota(jnp.int32, (1, LANE), 1)
    back_x = lax.broadcasted_iota(jnp.int32, (LANE, rest), 0)
    back_t = lax.broadcasted_iota(jnp.int32, (LANE, rest), 1)

    spec_copy.wait()
    for c in range(chunks):
        lo, hi = bounds[c]

        def widen(i, carry):
            n = lax.rem(i, per_tile)
            back = jnp.where(back_x == back_t + n * rest, 1.0, 0.0).astype(jnp.bfloat16)
            expand[lo + i] = jnp.dot(
                back, spec[lo + i, main:, :], preferred_element_type=jnp.float32
            ).astype(jnp.bfloat16)
            return carry

        lax.fori_loop(0, hi - lo, widen, 0)

    def fourier(c):
        lo, hi = bounds[c]

        for i in range(hi - lo):
            s = lo + i
            p = wp_ref[wi * slots + s]
            par = jnp.bitwise_and(p, 1)
            border = wave_count - p

            def split(values, fold_rows):
                low = jnp.where(fold_rows < border, 1, 0)
                even = jnp.where(low != par, 1.0, 0.0).astype(jnp.bfloat16)
                picked = values * even
                return jnp.concatenate([picked, values - picked], axis=0)

            lg = split(leg[:, s].reshape(qtot, main), cols)
            tile = tail[:, c, i // per_tile].reshape(qtot, LANE)
            lt = split(tile, main + tcols - i % per_tile * rest)
            f = jnp.dot(lg, spec[s, :main, :], preferred_element_type=jnp.float32)
            f = f + jnp.dot(lt, expand[s], preferred_element_type=jnp.float32)
            g = jnp.dot(f.astype(jnp.bfloat16), perm, preferred_element_type=jnp.float32)
            for h in range(2):
                stage[pl.ds(h * CH + i, qtot, stride=2 * CH), :] = g[h * qtot : (h + 1) * qtot]

        snd[c] = stage[...].astype(jnp.bfloat16).reshape(snd.shape[1:])

    leg_copy.wait()
    polls = [(k, c) for k in range(nl - 1) for c in range(chunks)]
    early = len(polls) - chunks
    done = 0
    for n, (k, c) in enumerate(polls[:early]):
        upto = rows * (n + 1) // (early + 1)
        basis_rows(done, upto)
        done = upto
        arrive(k, c)
    basis_rows(done, rows)
    keeps = []
    for c in range(chunks):
        arrive(nl - 2, c)
        fourier(c)
        for d in range(1, nw):
            aa(c, d).start()
        keep = pltpu.make_async_copy(snd.at[c, wi], rcv.at[c, wi], own_sem.at[c])
        keep.start()
        keeps.append(keep)

    def landed(c):
        keeps[c].wait()
        for d in range(1, nw):
            aa(c, d).wait_recv()

    def product(c, r, par):
        weight = amp[r, par, c * kchunk : (c + 1) * kchunk, :]
        v = rcv[c, :, r, par].reshape(kchunk, items) * weight
        vt = v.T
        lhs = jnp.concatenate([vt[:layers], vt[layers:]], axis=1)
        rhs = basis[r, par, 2 * c * kchunk : 2 * (c + 1) * kchunk, :]
        return jnp.dot(lhs, rhs, preferred_element_type=jnp.float32)

    for c in range(chunks - 1):
        landed(c)

        def partial(r, carry):
            for par in range(2):
                value = product(c, r, par)
                part[r, par] = value if c == 0 else part[r, par] + value
            return carry

        lax.fori_loop(0, rows, partial, 0)

    lanes = lax.broadcasted_iota(jnp.int32, (layers, half_width), 1)
    landed(chunks - 1)

    def final(r, carry):
        half = lax.shift_right_logical(row_count(r), 1)
        sums = []
        for par in range(2):
            value = product(chunks - 1, r, par)
            sums.append(value if chunks == 1 else part[r, par] + value)
        inside = lanes < half
        first = jnp.where(inside, sums[0] + sums[1], 0.0)
        second = jnp.where(inside, sums[0] - sums[1], 0.0)
        blank = jnp.zeros_like(first)
        moved = pltpu.roll(jnp.concatenate([second, blank], axis=1), half, 1)
        whole = jnp.concatenate([first, blank], axis=1) + moved
        obuf[r] = whole[:, :width].astype(jnp.bfloat16)
        return carry

    lax.fori_loop(0, rows, final, 0)
    out_copy = pltpu.make_async_copy(obuf, out_ref, out_sem)
    out_copy.start()

    for c in range(chunks):
        for k in range(nl - 1):
            for way in range(2):
                going, block = sends(way, k)

                @pl.when(going)
                def _():
                    for piece in range(2):
                        hop(way, k, c, piece, block).wait_send()

        for d in range(1, nw):
            aa(c, d).wait_send()
    out_copy.wait()


def on_device(spectral, legendre, wave_pair, lat_slot):
    slots, fold, items = spectral.shape
    wave_count = fold - 1
    nw = lax.axis_size("wav")
    nl = lax.axis_size("lev")
    rows = lat_slot.shape[0] // nw
    layers = items // 2
    width = 2 * NLAT + 16
    half_width = -(-(width // 2) // LANE) * LANE
    main = fold // LANE * LANE
    per_tile = LANE // (fold - main)
    span = (CH // per_tile) * per_tile
    chunks = -(-slots // span)
    kdim = chunks * nw * CH
    leg_t = jnp.transpose(legendre, (0, 2, 1))
    lrows = leg_t.shape[1]

    smem = pl.BlockSpec(memory_space=pltpu.SMEM)
    hbm = pl.BlockSpec(memory_space=pl.ANY)
    dma = pltpu.SemaphoreType.DMA
    vmem = pltpu.VMEM
    half = jnp.bfloat16
    return pl.pallas_call(
        functools.partial(kernel, nw, nl, slots, wave_count, half_width),
        out_shape=jax.ShapeDtypeStruct((rows, layers, width), half),
        in_specs=[smem, smem, hbm, hbm],
        out_specs=hbm,
        scratch_shapes=[
            vmem((slots, fold, items), half),
            vmem((slots, lrows, fold), half),
            vmem((nl, slots, lrows, main), half),
            vmem((nl, chunks, CH // per_tile, lrows, LANE), half),
            vmem((slots, LANE, items), half),
            vmem((kdim, LANE), jnp.float32),
            vmem((rows, 2, kdim, LANE), half),
            vmem((rows, 2, 8, half_width), jnp.float32),
            vmem((rows, 2, layers, half_width), jnp.float32),
            vmem((nw * rows * 2 * CH, items), jnp.float32),
            vmem((chunks, nw, rows, 2, CH, items), half),
            vmem((chunks, nw, rows, 2, CH, items), half),
            vmem((rows, 2, 2 * kdim, half_width), half),
            vmem((rows, layers, width), half),
            dma((3,)),
            dma((2, nl - 1, chunks, 2)),
            dma((2, nl - 1, chunks, 2)),
            dma((chunks, nw)),
            dma((chunks, nw)),
            dma((chunks,)),
            dma,
        ],
        compiler_params=pltpu.CompilerParams(collective_id=0, has_side_effects=True),
    )(wave_pair, lat_slot, spectral, leg_t)


def solution(mesh):
    return jax.shard_map(
        on_device,
        mesh=mesh,
        in_specs=(P("wav", None, "lev"), P("wav", None, "lev"), P(), P()),
        out_specs=P("wav", "lev", None),
        check_vma=False,
    )
```

profile of v0, /device:TPU:0, one launch (start us, length us, event | category | flops | bytes accessed | tf_op | source)
XLA Modules:
  0.0 48.8 jit_solution(1522877790267202408)
XLA Ops:
  0.0 46.0 %shard_map.46 = bf16[8,64,1616]{2,1,0:T(8,128)(2,1)} custom-call(s32[200]{0:T(256)} %wp_ref.1, s32[64]{0:T(128)} %lat_ref.1, bf16[25,401,128]{2,1,0:T(8,128)(2,1)} %spec_ref.1, bf16[25,16,401]{2,1,0:T(8,128)(2,1)} %bitcast.1), custom_call_target="tpu_custom_call" | custom-call | tf_op jit(solution)/shard_map/pallas_call | solution.py:374
  46.1 2.8 %copy.6 = bf16[8,64,1616]{2,1,0:T(8,128)(2,1)} copy(bf16[8,64,1616]{2,1,0:T(8,128)(2,1)} %shard_map.46) | data formatting | bytes 3309568
where the time goes:
time: 49 us; the launch traced here: 48.8 us
  Pallas kernels  46 us (94%)
  local copies, waits for them, and re-layouts  2.76 us (6%)
    pallas_call x1, Pallas kernels, on_device(): pl.pallas_call(functools.partial(kernel, nw, nl, slots, wave_count, half_...  46 us
    unnamed x1, local copies, waits for them, and re-layouts  2.76 us

commit v1 on v0

v1 whole, which is shorter than its diff:
```python
import functools
import math

import jax
import jax.numpy as jnp
from jax import lax
from jax.experimental import pallas as pl
from jax.experimental.pallas import tpu as pltpu
from jax.sharding import PartitionSpec as P

NLAT = 800
LANE = 128
PACK = 4
HALVES = 2
SIDE = HALVES * PACK
KB = 64
ROW_STEP = 4
COLS = 256


def half_turn(x):
    u = x * math.pi
    v = u * u
    s = -2.5052108385441720e-08
    for coef in (2.7557319223985893e-06, -1.9841269841269841e-04, 8.3333333333333333e-03, -1.6666666666666667e-01, 1.0):
        s = s * v + coef
    s = s * u
    c = -2.7557319223985888e-07
    for coef in (2.4801587301587302e-05, -1.3888888888888889e-03, 4.1666666666666667e-02, -0.5, 1.0):
        c = c * v + coef
    return 1.0 - 2.0 * s * s, 2.0 * s * c


def trig(prod, count, inv):
    r = prod - jnp.floor(prod * inv + 0.5) * count
    return half_turn(r * inv)


def chunk_plan(slots, per_tile):
    bounds = []
    for lo in range(0, slots, per_tile):
        hi = min(slots, lo + per_tile)
        for start in range(lo, hi, PACK):
            bounds.append((start, min(hi, start + PACK)))
    return bounds


def group_plan(chunks):
    paired = max(0, chunks - 3) // 2 * 2
    return [(c, c + 1) for c in range(0, paired, 2)] + [(c,) for c in range(paired, chunks)]


def exchange_order(nw):
    if nw & (nw - 1):
        return list(range(1, nw))
    return sorted(range(1, nw), key=lambda k: (-bin(k >> 1).count("1"), k))


def partner(wi, k, nw, sending):
    if nw & (nw - 1):
        return lax.rem(wi + (k if sending else nw - k), nw)
    other = wi
    bit = 1
    while bit < nw:
        if k & bit:
            other = other + bit * (1 - 2 * lax.rem(lax.div(wi, bit), 2))
        bit *= 2
    return other


def kernel(
    nw, nl, slots, wave_count, bounds, groups, per_tile,
    wp_hbm, lat_hbm, spec_hbm, leg_hbm, out_ref,
    wp, lat, spec, own, leg, tail, wts, waves, stage, snd, rcv, basis, part,
    loc_sem, ag_send, ag_recv, aa_send, aa_recv,
):
    wi = lax.axis_index("wav")
    li = lax.axis_index("lev")
    chunks = len(bounds)
    rows, layers, width = out_ref.shape
    fold = spec.shape[1]
    main = leg.shape[3]
    rest = fold - main
    items = 2 * layers
    full = basis.shape[2]
    blocks = full // LANE
    kchunk = nw * SIDE
    qtot = nw * rows
    fmt = pl.DeviceIdType.MESH
    half = jnp.bfloat16

    copies = [
        pltpu.make_async_copy(src, dst, loc_sem.at[i])
        for i, (src, dst) in enumerate((
            (leg_hbm.at[:, :, pl.ds(0, main)], leg.at[li]),
            (leg_hbm, own),
            (wp_hbm, wp),
            (lat_hbm, lat),
            (spec_hbm, spec),
        ))
    ]
    for copy in copies:
        copy.start()
    leg_copy, own_copy, wp_copy, lat_copy, spec_copy = copies

    barrier = pltpu.get_barrier_semaphore()
    for step in (1, -1):
        @pl.when((li + step >= 0) & (li + step < nl))
        def _():
            pl.semaphore_signal(barrier, inc=1, device_id=(wi, li + step), device_id_type=fmt)
    order = exchange_order(nw)
    for k in order:
        pl.semaphore_signal(barrier, inc=1, device_id=(partner(wi, k, nw, True), li), device_id_type=fmt)
    beside = jnp.where(li > 0, 1, 0) + jnp.where(li < nl - 1, 1, 0)
    pl.semaphore_wait(barrier, beside + nw - 1)

    def fresh(c):
        lo, hi = bounds[c]
        return [t for t in range(tail.shape[1]) if lo <= t * per_tile < hi]

    def hops(way, k, c, block):
        lo, hi = bounds[c]
        views = [leg.at[block, pl.ds(lo, hi - lo)]] + [tail.at[block, t] for t in fresh(c)]
        return [
            pltpu.make_async_remote_copy(
                src_ref=view,
                dst_ref=view,
                send_sem=ag_send.at[way, k, c, n],
                recv_sem=ag_recv.at[way, k, c, n],
                device_id=(wi, li + 1 - 2 * way),
                device_id_type=fmt,
            )
            for n, view in enumerate(views)
        ]

    def sends(way, k):
        if way == 0:
            return (li - k >= 0) & (li + 1 < nl), jnp.maximum(li - k, 0)
        return (li + k < nl) & (li >= 1), jnp.minimum(li + k, nl - 1)

    def receives(way, k):
        if way == 0:
            return li - 1 - k >= 0, jnp.maximum(li - 1 - k, 0)
        return li + 1 + k < nl, jnp.minimum(li + 1 + k, nl - 1)

    def send(k, c, which=slice(None)):
        for way in range(2):
            going, block = sends(way, k)

            @pl.when(going)
            def _():
                for hop in hops(way, k, c, block)[which]:
                    hop.start()

    def arrive(k, c):
        for way in range(2):
            coming, block = receives(way, k)

            @pl.when(coming)
            def _():
                for hop in hops(way, k, c, block):
                    hop.wait_recv()

        if k + 1 < nl - 1:
            send(k + 1, c)

    def exchange(c, k):
        dest = partner(wi, k, nw, True)
        return pltpu.make_async_remote_copy(
            src_ref=snd.at[c, dest],
            dst_ref=rcv.at[c, wi],
            send_sem=aa_send.at[c, k],
            recv_sem=aa_recv.at[c, k],
            device_id=(dest, li),
            device_id_type=fmt,
        )

    leg_copy.wait()
    send(0, 0, slice(0, 1))
    own_copy.wait()
    place_t = lax.broadcasted_iota(jnp.int32, (rest, LANE), 0)
    place_x = lax.broadcasted_iota(jnp.int32, (rest, LANE), 1)
    for t in range(tail.shape[1]):
        total = jnp.zeros(tail.shape[2:], jnp.float32)
        for n in range(per_tile):
            s = t * per_tile + n
            if s < slots:
                place = jnp.where(place_x == place_t + n * rest, 1.0, 0.0).astype(half)
                total += jnp.dot(own[s, :, main:], place, preferred_element_type=jnp.float32)
        tail[li, t] = total.astype(half)
    send(0, 0, slice(1, None))
    ahead = chunks // 2 + 1
    for c in range(1, ahead):
        send(0, c)

    waves[...] = jnp.full_like(waves, -1.0)
    wp_copy.wait()
    lat_copy.wait()

    def place_waves(src, carry):
        for c, (lo, hi) in enumerate(bounds):
            for s in range(lo, hi):
                p = wp[src * slots + s]
                for h in range(HALVES):
                    m = jnp.where(p < 0, -1, p if h == 0 else wave_count - 1 - p).astype(jnp.float32)
                    row = c * kchunk + src * SIDE + h * PACK + s - lo
                    waves[pl.ds(row, 1), :] = jnp.full((1, LANE), m, jnp.float32)
        return carry

    lax.fori_loop(0, nw, place_waves, 0)

    stage[...] = jnp.zeros_like(stage)
    out_i = lax.broadcasted_iota(jnp.int32, (items, items), 1)
    in_i = lax.broadcasted_iota(jnp.int32, (items, items), 0)
    perm = jnp.where(
        in_i == jnp.where(out_i < layers, 2 * out_i, 2 * (out_i - layers) + 1), 1.0, 0.0
    ).astype(half)
    back_x = lax.broadcasted_iota(jnp.int32, (LANE, rest), 0)
    back_t = lax.broadcasted_iota(jnp.int32, (LANE, rest), 1)

    def weigh(s, carry):
        n = lax.rem(s, per_tile)
        wts[s, :main, :] = jnp.dot(spec[s, :main, :], perm, preferred_element_type=jnp.float32).astype(half)
        back = jnp.where(back_x == back_t + n * rest, 1.0, 0.0).astype(half)
        tails = jnp.dot(spec[s, main:, :], perm, preferred_element_type=jnp.float32).astype(half)
        wts[s, main:, :] = jnp.dot(back, tails, preferred_element_type=jnp.float32).astype(half)
        return carry

    fine = lax.broadcasted_iota(jnp.int32, (KB, LANE), 1).astype(jnp.float32)
    lane = lax.broadcasted_iota(jnp.int32, (KB, LANE), 1)
    pieces = kchunk // KB
    steps = rows // ROW_STEP

    def row_count(r):
        a = lat[wi * rows + r]
        return 20 + 4 * jnp.minimum(a, NLAT - 1 - a)

    def basis_rows(c):
        for group, start in zip(groups, group_starts):
            if c in group:
                real = start + group.index(c) * kchunk
                return real, real + len(group) * kchunk

    group_starts = []
    for group in groups:
        group_starts.append(2 * kchunk * sum(len(g) for g in groups[: len(group_starts)]))

    def make_basis(c, unit):
        real0, imag0 = basis_rows(c)
        piece = lax.div(unit, steps)
        r0 = lax.rem(unit, steps) * ROW_STEP
        k0 = pl.multiple_of(piece * KB, KB)
        m = waves[pl.ds(pl.multiple_of(c * kchunk + k0, KB), KB), :]
        counts = [row_count(r0 + i) for i in range(ROW_STEP)]
        each = jnp.full((KB, LANE), counts[0].astype(jnp.float32), jnp.float32)
        for i in range(1, ROW_STEP):
            each = jnp.where(lane == i, counts[i].astype(jnp.float32), each)
        stride_cos, stride_sin = trig(m * LANE, each, 1.0 / each)
        for i in range(ROW_STEP):
            r = r0 + i
            highest = jnp.minimum(wave_count - 1, lax.shift_right_logical(counts[i] - 1, 1)).astype(jnp.float32)
            count = jnp.full((KB, LANE), counts[i].astype(jnp.float32), jnp.float32)
            factor = jnp.where((m >= 0.0) & (m <= highest), jnp.where(m == 0.0, 1.0, 2.0), 0.0)
            sc = jnp.broadcast_to(stride_cos[:, i : i + 1], (KB, LANE))
            ss = jnp.broadcast_to(stride_sin[:, i : i + 1], (KB, LANE))
            c0, s0 = trig(m * fine, count, 1.0 / count)
            c0 = c0 * factor
            s0 = -(s0 * factor)
            c1 = c0 * sc + s0 * ss
            s1 = s0 * sc - c0 * ss
            twice = sc + sc
            for b in range(blocks):
                cols = slice(b * LANE, (b + 1) * LANE)
                basis[r, pl.ds(real0 + k0, KB), cols] = c0.astype(half)
                basis[r, pl.ds(imag0 + k0, KB), cols] = s0.astype(half)
                if b + 1 < blocks:
                    c0, c1 = c1, twice * c1 - c0
                    s0, s1 = s1, twice * s1 - s0

    def basis_for(c):
        def body(unit, carry):
            make_basis(c, unit)
            return carry

        lax.fori_loop(0, pieces * steps, body, 0)

    cols = lax.broadcasted_iota(jnp.int32, (1, main), 1)
    tcols = lax.broadcasted_iota(jnp.int32, (1, LANE), 1)

    def fourier(c):
        lo, hi = bounds[c]
        for s in range(lo, hi):
            border = wave_count - wp[wi * slots + s]
            fold_rows = jnp.concatenate([cols, main + tcols - s % per_tile * rest], axis=1)
            low = jnp.where(fold_rows < border, 1.0, 0.0).astype(half)
            values = jnp.concatenate([
                leg[:, s].reshape(qtot, main),
                tail[:, s // per_tile].reshape(qtot, LANE),
            ], axis=1)
            picked = values * low
            f = jnp.dot(
                jnp.concatenate([picked, values - picked], axis=0), wts[s],
                preferred_element_type=jnp.float32,
            )
            for h in range(HALVES):
                stage[pl.ds(h * PACK + s - lo, qtot, stride=SIDE), :] = f[h * qtot : (h + 1) * qtot]
        snd[c] = stage[...].astype(half).reshape(snd.shape[1:])
        for k in order:
            exchange(c, k).start()
        mine = stage[pl.ds(pl.multiple_of(wi * rows * SIDE, rows * SIDE), rows * SIDE), :]
        rcv[c, wi] = mine.astype(half).reshape(rcv.shape[2:])

    def landed(c):
        for k in order:
            exchange(c, k).wait_recv()

    lanes = lax.broadcasted_iota(jnp.int32, (layers, COLS), 1)

    def synthesis(g):
        group = groups[g]
        for c in group:
            landed(c)
        depth = 2 * kchunk * len(group)

        def body(r, carry):
            v = jnp.concatenate([rcv[c, :, r].reshape(kchunk, items) for c in group], axis=0)
            vt = v.T
            lhs = jnp.concatenate([vt[:layers], vt[layers:]], axis=1)
            count = row_count(r)
            for n0 in range(0, full, COLS):
                n1 = min(full, n0 + COLS)
                rhs = basis[r, group_starts[g] : group_starts[g] + depth, n0:n1]
                value = jnp.dot(lhs, rhs, preferred_element_type=jnp.float32)
                if g:
                    value = part[r, :, n0:n1] + value
                if g + 1 < len(groups):
                    part[r, :, n0:n1] = value
                else:
                    value = jnp.where(lanes[:, : n1 - n0] + n0 < count, value, 0.0)
                    stop = min(width, n1)
                    out_ref[r, :, n0:stop] = value[:, : stop - n0].astype(half)
            return carry

        lax.fori_loop(0, rows, body, 0, unroll=2)

    spec_copy.wait()
    lax.fori_loop(0, slots, weigh, 0)

    polls = sorted(((k, c) for k in range(nl - 1) for c in range(chunks)), key=lambda p: (p[0] + p[1], p[0]))
    made = 0
    ready = 0
    shown = 0
    for k, c in polls:
        arrive(k, c)
        if k == 0 and ahead < chunks:
            send(0, ahead)
            ahead += 1
        if k == nl - 2:
            fourier(c)
            ready = c + 1
            while shown < len(groups) and groups[shown][-1] + 3 <= c:
                synthesis(shown)
                shown += 1
        if made < chunks:
            basis_for(made)
            made += 1
    while made < chunks:
        basis_for(made)
        made += 1
    while shown < len(groups):
        synthesis(shown)
        shown += 1

    for c in range(chunks):
        for k in range(nl - 1):
            for way in range(2):
                going, block = sends(way, k)

                @pl.when(going)
                def _():
                    for hop in hops(way, k, c, block):
                        hop.wait_send()

        for k in order:
            exchange(c, k).wait_send()


def on_device(spectral, legendre, wave_pair, lat_slot):
    slots, fold, items = spectral.shape
    wave_count = fold - 1
    nw = lax.axis_size("wav")
    nl = lax.axis_size("lev")
    rows = lat_slot.shape[0] // nw
    layers = items // 2
    width = 2 * NLAT + 16
    full = -(-width // LANE) * LANE
    main = fold // LANE * LANE
    per_tile = LANE // (fold - main)
    bounds = chunk_plan(slots, per_tile)
    chunks = len(bounds)
    groups = group_plan(chunks)
    tiles = -(-slots // per_tile)
    leg_t = jnp.transpose(legendre, (0, 2, 1))
    lrows = leg_t.shape[1]
    kchunk = nw * SIDE

    hbm = pl.BlockSpec(memory_space=pl.ANY)
    dma = pltpu.SemaphoreType.DMA
    vmem = pltpu.VMEM
    half = jnp.bfloat16
    place = functools.partial(pltpu.with_memory_space_constraint, memory_space=pltpu.HBM)
    return pl.pallas_call(
        functools.partial(kernel, nw, nl, slots, wave_count, bounds, groups, per_tile),
        out_shape=vmem((rows, layers, width), half),
        in_specs=[hbm, hbm, hbm, hbm],
        out_specs=pl.BlockSpec(memory_space=vmem),
        scratch_shapes=[
            pltpu.SMEM(wave_pair.shape, jnp.int32),
            pltpu.SMEM(lat_slot.shape, jnp.int32),
            vmem((slots, fold, items), half),
            vmem((slots, lrows, fold), half),
            vmem((nl, slots, lrows, main), half),
            vmem((nl, tiles, lrows, LANE), half),
            vmem((slots, main + LANE, items), half),
            vmem((chunks * kchunk, LANE), jnp.float32),
            vmem((nw * rows * SIDE, items), jnp.float32),
            vmem((chunks, nw, rows, SIDE, items), half),
            vmem((chunks, nw, rows, SIDE, items), half),
            vmem((rows, 2 * chunks * kchunk, full), half),
            vmem((rows, layers, full), jnp.float32),
            dma((5,)),
            dma((2, nl - 1, chunks, 2)),
            dma((2, nl - 1, chunks, 2)),
            dma((chunks, nw)),
            dma((chunks, nw)),
        ],
        compiler_params=pltpu.CompilerParams(collective_id=0, has_side_effects=True, vmem_limit_bytes=52 << 20),
    )(place(wave_pair), place(lat_slot), place(spectral), place(leg_t))


def solution(mesh):
    return jax.shard_map(
        on_device,
        mesh=mesh,
        in_specs=(P("wav", None, "lev"), P("wav", None, "lev"), P(), P()),
        out_specs=P("wav", "lev", None),
        check_vma=False,
    )
```

time: 49 us -> 44.5 us (0.908)
  Pallas kernels: 46 us -> 43.2 us
  local copies, waits for them, and re-layouts: 2.76 us -> 1.19 us
    pallas_call x1, Pallas kernels: 46 us -> 43.2 us  [on_device(): pl.pallas_call(functools.partial(kernel, nw, nl, slots, wave_count, bound...]
    unnamed x1, local copies, waits for them, and re-layouts: 2.76 us -> 1.19 us
where the time goes in v1:
time: 44.5 us; the launch traced here: 44.4 us
  Pallas kernels  43.2 us (97%)
  local copies, waits for them, and re-layouts  1.19 us (3%)
    pallas_call x1, Pallas kernels, on_device(): pl.pallas_call(functools.partial(kernel, nw, nl, slots, wave_count, bound...  43.2 us
    unnamed x1, local copies, waits for them, and re-layouts  1.19 us

profile of v1, /device:TPU:0, one launch (start us, length us, event | category | flops | bytes accessed | tf_op | source)
XLA Modules:
  0.0 44.4 jit_solution(10811121773993002183)
XLA Ops:
  0.0 43.2 %shard_map.46 = bf16[8,64,1616]{2,1,0:T(8,128)(2,1)S(1)} custom-call(s32[200]{0:T(256)} %wp_hbm.1, s32[64]{0:T(128)} %lat_hbm.1, bf16[25,401,128]{2,1,0:T(8,128)(2,1)} %spec_hbm.1, bf16[25,16,401]{2,1,0:T(8,128)(2,1)} %bitcast.1), custom_call_target="tpu_custom_call" | custom-call | tf_op jit(solution)/shard_map/pallas_call | solution.py:412
  43.2 1.2 %copy.6 = bf16[8,64,1616]{2,1,0:T(8,128)(2,1)} copy(bf16[8,64,1616]{2,1,0:T(8,128)(2,1)S(1)} %shard_map.46) | data formatting | bytes 3309568

commit v2 on v1

--- a/solution.py
+++ b/solution.py
@@ -118,9 +118,9 @@
         lo, hi = bounds[c]
         return [t for t in range(tail.shape[1]) if lo <= t * per_tile < hi]
 
-    def hops(way, k, c, block):
+    def hops(way, k, c, block, pieces=(0, 1)):
         lo, hi = bounds[c]
-        views = [leg.at[block, pl.ds(lo, hi - lo)]] + [tail.at[block, t] for t in fresh(c)]
+        views = [(0, leg.at[block, pl.ds(lo, hi - lo)])] + [(1, tail.at[block, t]) for t in fresh(c)]
         return [
             pltpu.make_async_remote_copy(
                 src_ref=view,
@@ -130,7 +130,8 @@
                 device_id=(wi, li + 1 - 2 * way),
                 device_id_type=fmt,
             )
-            for n, view in enumerate(views)
+            for n, view in views
+            if n in pieces
         ]
 
     def sends(way, k):
@@ -143,13 +144,13 @@
             return li - 1 - k >= 0, jnp.maximum(li - 1 - k, 0)
         return li + 1 + k < nl, jnp.minimum(li + 1 + k, nl - 1)
 
-    def send(k, c, which=slice(None)):
+    def send(k, c, pieces=(0, 1)):
         for way in range(2):
             going, block = sends(way, k)
 
             @pl.when(going)
             def _():
-                for hop in hops(way, k, c, block)[which]:
+                for hop in hops(way, k, c, block, pieces):
                     hop.start()
 
     def arrive(k, c):
@@ -176,7 +177,7 @@
         )
 
     leg_copy.wait()
-    send(0, 0, slice(0, 1))
+    send(0, 0, (0,))
     own_copy.wait()
     place_t = lax.broadcasted_iota(jnp.int32, (rest, LANE), 0)
     place_x = lax.broadcasted_iota(jnp.int32, (rest, LANE), 1)
@@ -188,8 +189,8 @@
                 place = jnp.where(place_x == place_t + n * rest, 1.0, 0.0).astype(half)
                 total += jnp.dot(own[s, :, main:], place, preferred_element_type=jnp.float32)
         tail[li, t] = total.astype(half)
-    send(0, 0, slice(1, None))
-    ahead = chunks // 2 + 1
+    send(0, 0, (1,))
+    ahead = min(chunks, 3)
     for c in range(1, ahead):
         send(0, c)
 
@@ -218,13 +219,12 @@
     back_x = lax.broadcasted_iota(jnp.int32, (LANE, rest), 0)
     back_t = lax.broadcasted_iota(jnp.int32, (LANE, rest), 1)
 
-    def weigh(s, carry):
-        n = lax.rem(s, per_tile)
+    def weigh(s):
+        n = s % per_tile
         wts[s, :main, :] = jnp.dot(spec[s, :main, :], perm, preferred_element_type=jnp.float32).astype(half)
         back = jnp.where(back_x == back_t + n * rest, 1.0, 0.0).astype(half)
         tails = jnp.dot(spec[s, main:, :], perm, preferred_element_type=jnp.float32).astype(half)
         wts[s, main:, :] = jnp.dot(back, tails, preferred_element_type=jnp.float32).astype(half)
-        return carry
 
     fine = lax.broadcasted_iota(jnp.int32, (KB, LANE), 1).astype(jnp.float32)
     lane = lax.broadcasted_iota(jnp.int32, (KB, LANE), 1)
@@ -247,10 +247,9 @@
 
     def make_basis(c, unit):
         real0, imag0 = basis_rows(c)
-        piece = lax.div(unit, steps)
-        r0 = lax.rem(unit, steps) * ROW_STEP
-        k0 = pl.multiple_of(piece * KB, KB)
-        m = waves[pl.ds(pl.multiple_of(c * kchunk + k0, KB), KB), :]
+        k0 = unit // steps * KB
+        r0 = unit % steps * ROW_STEP
+        m = waves[c * kchunk + k0 : c * kchunk + k0 + KB, :]
         counts = [row_count(r0 + i) for i in range(ROW_STEP)]
         each = jnp.full((KB, LANE), counts[0].astype(jnp.float32), jnp.float32)
         for i in range(1, ROW_STEP):
@@ -271,18 +270,11 @@
             twice = sc + sc
             for b in range(blocks):
                 cols = slice(b * LANE, (b + 1) * LANE)
-                basis[r, pl.ds(real0 + k0, KB), cols] = c0.astype(half)
-                basis[r, pl.ds(imag0 + k0, KB), cols] = s0.astype(half)
+                basis[r, real0 + k0 : real0 + k0 + KB, cols] = c0.astype(half)
+                basis[r, imag0 + k0 : imag0 + k0 + KB, cols] = s0.astype(half)
                 if b + 1 < blocks:
                     c0, c1 = c1, twice * c1 - c0
                     s0, s1 = s1, twice * s1 - s0
-
-    def basis_for(c):
-        def body(unit, carry):
-            make_basis(c, unit)
-            return carry
-
-        lax.fori_loop(0, pieces * steps, body, 0)
 
     cols = lax.broadcasted_iota(jnp.int32, (1, main), 1)
     tcols = lax.broadcasted_iota(jnp.int32, (1, LANE), 1)
@@ -343,12 +335,23 @@
 
         lax.fori_loop(0, rows, body, 0, unroll=2)
 
+    units = [(c, unit) for c in range(chunks) for unit in range(pieces * steps)]
+    pace = -(-slots // len(units))
+    done = {"weighed": 0, "made": 0}
+
+    def prepare(upto):
+        while done["weighed"] < min(slots, upto):
+            weigh(done["weighed"])
+            done["weighed"] += 1
+
+    def work(upto):
+        while done["made"] < min(len(units), upto):
+            prepare(done["weighed"] + pace)
+            make_basis(*units[done["made"]])
+            done["made"] += 1
+
     spec_copy.wait()
-    lax.fori_loop(0, slots, weigh, 0)
-
     polls = sorted(((k, c) for k in range(nl - 1) for c in range(chunks)), key=lambda p: (p[0] + p[1], p[0]))
-    made = 0
-    ready = 0
     shown = 0
     for k, c in polls:
         arrive(k, c)
@@ -356,17 +359,14 @@
             send(0, ahead)
             ahead += 1
         if k == nl - 2:
+            prepare(bounds[c][1])
             fourier(c)
-            ready = c + 1
             while shown < len(groups) and groups[shown][-1] + 3 <= c:
+                work(len(units) // chunks * (groups[shown][-1] + 1))
                 synthesis(shown)
                 shown += 1
-        if made < chunks:
-            basis_for(made)
-            made += 1
-    while made < chunks:
-        basis_for(made)
-        made += 1
+        work(done["made"] + 1)
+    work(len(units))
     while shown < len(groups):
         synthesis(shown)
         shown += 1

time: 44.5 us -> 39.9 us (0.90)
  Pallas kernels: 43.2 us -> 38.6 us
    pallas_call x1, Pallas kernels: 43.2 us -> 38.6 us  [on_device(): pl.pallas_call(functools.partial(kernel, nw, nl, slots, wave_count, bound...]
where the time goes in v2:
time: 39.9 us; the launch traced here: 39.8 us
  Pallas kernels  38.6 us (97%)
  local copies, waits for them, and re-layouts  1.19 us (3%)
    pallas_call x1, Pallas kernels, on_device(): pl.pallas_call(functools.partial(kernel, nw, nl, slots, wave_count, bound...  38.6 us
    unnamed x1, local copies, waits for them, and re-layouts  1.19 us

profile of v2, /device:TPU:0, one launch (start us, length us, event | category | flops | bytes accessed | tf_op | source)
XLA Modules:
  0.0 39.8 jit_solution(12376254848025744125)
XLA Ops:
  0.0 38.6 %shard_map.46 = bf16[8,64,1616]{2,1,0:T(8,128)(2,1)S(1)} custom-call(s32[200]{0:T(256)} %wp_hbm.1, s32[64]{0:T(128)} %lat_hbm.1, bf16[25,401,128]{2,1,0:T(8,128)(2,1)} %spec_hbm.1, bf16[25,16,401]{2,1,0:T(8,128)(2,1)} %bitcast.1), custom_call_target="tpu_custom_call" | custom-call | tf_op jit(solution)/shard_map/pallas_call | solution.py:412
  38.6 1.2 %copy.6 = bf16[8,64,1616]{2,1,0:T(8,128)(2,1)} copy(bf16[8,64,1616]{2,1,0:T(8,128)(2,1)S(1)} %shard_map.46) | data formatting | bytes 3309568

commit v3 on v2

--- a/solution.py
+++ b/solution.py
@@ -82,8 +82,8 @@
     main = leg.shape[3]
     rest = fold - main
     items = 2 * layers
-    full = basis.shape[2]
-    blocks = full // LANE
+    blocks = basis.shape[1]
+    full = blocks * LANE
     kchunk = nw * SIDE
     qtot = nw * rows
     fmt = pl.DeviceIdType.MESH
@@ -269,9 +269,8 @@
             s1 = s0 * sc - c0 * ss
             twice = sc + sc
             for b in range(blocks):
-                cols = slice(b * LANE, (b + 1) * LANE)
-                basis[r, real0 + k0 : real0 + k0 + KB, cols] = c0.astype(half)
-                basis[r, imag0 + k0 : imag0 + k0 + KB, cols] = s0.astype(half)
+                basis[r, b, real0 + k0 : real0 + k0 + KB, :] = c0.astype(half)
+                basis[r, b, imag0 + k0 : imag0 + k0 + KB, :] = s0.astype(half)
                 if b + 1 < blocks:
                     c0, c1 = c1, twice * c1 - c0
                     s0, s1 = s1, twice * s1 - s0
@@ -321,7 +320,10 @@
             count = row_count(r)
             for n0 in range(0, full, COLS):
                 n1 = min(full, n0 + COLS)
-                rhs = basis[r, group_starts[g] : group_starts[g] + depth, n0:n1]
+                rhs = jnp.concatenate([
+                    basis[r, b, group_starts[g] : group_starts[g] + depth, :]
+                    for b in range(n0 // LANE, n1 // LANE)
+                ], axis=1)
                 value = jnp.dot(lhs, rhs, preferred_element_type=jnp.float32)
                 if g:
                     value = part[r, :, n0:n1] + value
@@ -333,7 +335,7 @@
                     out_ref[r, :, n0:stop] = value[:, : stop - n0].astype(half)
             return carry
 
-        lax.fori_loop(0, rows, body, 0, unroll=2)
+        lax.fori_loop(0, rows, body, 0, unroll=True)
 
     units = [(c, unit) for c in range(chunks) for unit in range(pieces * steps)]
     pace = -(-slots // len(units))
@@ -426,7 +428,7 @@
             vmem((nw * rows * SIDE, items), jnp.float32),
             vmem((chunks, nw, rows, SIDE, items), half),
             vmem((chunks, nw, rows, SIDE, items), half),
-            vmem((rows, 2 * chunks * kchunk, full), half),
+            vmem((rows, full // LANE, 2 * chunks * kchunk, LANE), half),
             vmem((rows, layers, full), jnp.float32),
             dma((5,)),
             dma((2, nl - 1, chunks, 2)),

time: 39.9 us -> 36.2 us (0.907)
  Pallas kernels: 38.6 us -> 34.8 us
    pallas_call x1, Pallas kernels: 38.6 us -> 34.8 us  [on_device(): pl.pallas_call(functools.partial(kernel, nw, nl, slots, wave_count, bound...]
where the time goes in v3:
time: 36.2 us; the launch traced here: 36 us
  Pallas kernels  34.8 us (96%)
  local copies, waits for them, and re-layouts  1.19 us (3%)
    pallas_call x1, Pallas kernels, on_device(): pl.pallas_call(functools.partial(kernel, nw, nl, slots, wave_count, bound...  34.8 us
    unnamed x1, local copies, waits for them, and re-layouts  1.19 us

profile of v3, /device:TPU:0, one launch (start us, length us, event | category | flops | bytes accessed | tf_op | source)
XLA Modules:
  0.0 36.0 jit_solution(7821636650840298419)
XLA Ops:
  0.0 34.8 %shard_map.46 = bf16[8,64,1616]{2,1,0:T(8,128)(2,1)S(1)} custom-call(s32[200]{0:T(256)} %wp_hbm.1, s32[64]{0:T(128)} %lat_hbm.1, bf16[25,401,128]{2,1,0:T(8,128)(2,1)} %spec_hbm.1, bf16[25,16,401]{2,1,0:T(8,128)(2,1)} %bitcast.1), custom_call_target="tpu_custom_call" | custom-call | tf_op jit(solution)/shard_map/pallas_call | solution.py:414
  34.8 1.2 %copy.6 = bf16[8,64,1616]{2,1,0:T(8,128)(2,1)} copy(bf16[8,64,1616]{2,1,0:T(8,128)(2,1)S(1)} %shard_map.46) | data formatting | bytes 3309568

commit v4 on v3

--- a/solution.py
+++ b/solution.py
@@ -56,6 +56,10 @@
     return sorted(range(1, nw), key=lambda k: (-bin(k >> 1).count("1"), k))
 
 
+def near(k):
+    return bin(k >> 1).count("1") <= 1
+
+
 def partner(wi, k, nw, sending):
     if nw & (nw - 1):
         return lax.rem(wi + (k if sending else nw - k), nw)
@@ -72,7 +76,7 @@
     nw, nl, slots, wave_count, bounds, groups, per_tile,
     wp_hbm, lat_hbm, spec_hbm, leg_hbm, out_ref,
     wp, lat, spec, own, leg, tail, wts, waves, stage, snd, rcv, basis, part,
-    loc_sem, ag_send, ag_recv, aa_send, aa_recv,
+    loc_sem, ag_send, main_recv, tail_recv, aa_send, aa_recv, *gate,
 ):
     wi = lax.axis_index("wav")
     li = lax.axis_index("lev")
@@ -109,30 +113,47 @@
         def _():
             pl.semaphore_signal(barrier, inc=1, device_id=(wi, li + step), device_id_type=fmt)
     order = exchange_order(nw)
-    for k in order:
+    first = [k for k in order if near(k)] if gate else order
+    for k in first:
         pl.semaphore_signal(barrier, inc=1, device_id=(partner(wi, k, nw, True), li), device_id_type=fmt)
     beside = jnp.where(li > 0, 1, 0) + jnp.where(li < nl - 1, 1, 0)
-    pl.semaphore_wait(barrier, beside + nw - 1)
+    pl.semaphore_wait(barrier, beside + len(first))
+    direct = [k for k in first if not k & 1]
+
+    def relay(stage):
+        for k in direct:
+            pl.semaphore_signal(gate[0].at[stage], inc=1, device_id=(partner(wi, k, nw, True), li), device_id_type=fmt)
+
+    def everyone():
+        for stage in range(len(direct) - 1 if gate else 0):
+            pl.semaphore_wait(gate[0].at[stage], len(direct))
+            if stage + 1 < len(direct) - 1:
+                relay(stage + 1)
 
     def fresh(c):
         lo, hi = bounds[c]
         return [t for t in range(tail.shape[1]) if lo <= t * per_tile < hi]
 
-    def hops(way, k, c, block, pieces=(0, 1)):
+    def hop(way, k, view, piece, recv):
+        return pltpu.make_async_remote_copy(
+            src_ref=view,
+            dst_ref=view,
+            send_sem=ag_send.at[way, k, piece],
+            recv_sem=recv,
+            device_id=(wi, li + 1 - 2 * way),
+            device_id_type=fmt,
+        )
+
+    def main_hop(way, k, c, blocks):
         lo, hi = bounds[c]
-        views = [(0, leg.at[block, pl.ds(lo, hi - lo)])] + [(1, tail.at[block, t]) for t in fresh(c)]
-        return [
-            pltpu.make_async_remote_copy(
-                src_ref=view,
-                dst_ref=view,
-                send_sem=ag_send.at[way, k, c, n],
-                recv_sem=ag_recv.at[way, k, c, n],
-                device_id=(wi, li + 1 - 2 * way),
-                device_id_type=fmt,
-            )
-            for n, view in views
-            if n in pieces
-        ]
+        return hop(way, k, leg.at[blocks, pl.ds(lo, hi - lo)], 0, main_recv.at[k, c])
+
+    def tail_hop(way, k, t, blocks):
+        return hop(way, k, tail.at[blocks, t], 1, tail_recv.at[k, t])
+
+    def hops(way, k, c, blocks, pieces=(0, 1)):
+        chosen = [main_hop(way, k, c, blocks)] if 0 in pieces else []
+        return chosen + ([tail_hop(way, k, t, blocks) for t in fresh(c)] if 1 in pieces else [])
 
     def sends(way, k):
         if way == 0:
@@ -154,13 +175,13 @@
                     hop.start()
 
     def arrive(k, c):
-        for way in range(2):
-            coming, block = receives(way, k)
-
-            @pl.when(coming)
+        from_low, _ = receives(0, k)
+        from_high, _ = receives(1, k)
+        for come, number in ((from_low & from_high, 2), (from_low != from_high, 1)):
+            @pl.when(come)
             def _():
-                for hop in hops(way, k, c, block):
-                    hop.wait_recv()
+                for copy in hops(0, k, c, pl.ds(0, number)):
+                    copy.wait_recv()
 
         if k + 1 < nl - 1:
             send(k + 1, c)
@@ -168,11 +189,21 @@
     def exchange(c, k):
         dest = partner(wi, k, nw, True)
         return pltpu.make_async_remote_copy(
-            src_ref=snd.at[c, dest],
+            src_ref=snd.at[c * nw + dest],
             dst_ref=rcv.at[c, wi],
-            send_sem=aa_send.at[c, k],
-            recv_sem=aa_recv.at[c, k],
+            send_sem=aa_send.at[0],
+            recv_sem=aa_recv.at[c],
             device_id=(dest, li),
+            device_id_type=fmt,
+        )
+
+    def exchanged(c, src, dst):
+        return pltpu.make_async_remote_copy(
+            src_ref=src,
+            dst_ref=dst,
+            send_sem=aa_send.at[0],
+            recv_sem=aa_recv.at[c],
+            device_id=(partner(wi, 1, nw, True), li),
             device_id_type=fmt,
         )
 
@@ -193,6 +224,8 @@
     ahead = min(chunks, 3)
     for c in range(1, ahead):
         send(0, c)
+    if gate:
+        relay(0)
 
     waves[...] = jnp.full_like(waves, -1.0)
     wp_copy.wait()
@@ -295,15 +328,15 @@
             )
             for h in range(HALVES):
                 stage[pl.ds(h * PACK + s - lo, qtot, stride=SIDE), :] = f[h * qtot : (h + 1) * qtot]
-        snd[c] = stage[...].astype(half).reshape(snd.shape[1:])
+        snd[c * nw : (c + 1) * nw] = stage[...].astype(half).reshape((nw,) + snd.shape[1:])
         for k in order:
             exchange(c, k).start()
         mine = stage[pl.ds(pl.multiple_of(wi * rows * SIDE, rows * SIDE), rows * SIDE), :]
         rcv[c, wi] = mine.astype(half).reshape(rcv.shape[2:])
 
     def landed(c):
-        for k in order:
-            exchange(c, k).wait_recv()
+        others = pl.ds(0, nw - 1)
+        exchanged(c, rcv.at[c, others], rcv.at[c, others]).wait_recv()
 
     lanes = lax.broadcasted_iota(jnp.int32, (layers, COLS), 1)
 
@@ -362,6 +395,8 @@
             ahead += 1
         if k == nl - 2:
             prepare(bounds[c][1])
+            if c == 0:
+                everyone()
             fourier(c)
             while shown < len(groups) and groups[shown][-1] + 3 <= c:
                 work(len(units) // chunks * (groups[shown][-1] + 1))
@@ -373,18 +408,17 @@
         synthesis(shown)
         shown += 1
 
-    for c in range(chunks):
-        for k in range(nl - 1):
-            for way in range(2):
-                going, block = sends(way, k)
-
-                @pl.when(going)
-                def _():
-                    for hop in hops(way, k, c, block):
-                        hop.wait_send()
-
-        for k in order:
-            exchange(c, k).wait_send()
+    for k in range(nl - 1):
+        for way in range(2):
+            going, block = sends(way, k)
+
+            @pl.when(going)
+            def _():
+                hop(way, k, leg.at[block], 0, main_recv.at[k, 0]).wait_send()
+                hop(way, k, tail.at[block], 1, tail_recv.at[k, 0]).wait_send()
+
+    sent = snd.at[pl.ds(0, chunks * (nw - 1))]
+    exchanged(0, sent, sent).wait_send()
 
 
 def on_device(spectral, legendre, wave_pair, lat_slot):
@@ -405,6 +439,10 @@
     leg_t = jnp.transpose(legendre, (0, 2, 1))
     lrows = leg_t.shape[1]
     kchunk = nw * SIDE
+
+    bits = (nw >> 1).bit_length() - 1
+    staged = nw & (nw - 1) == 0 and bits > 1
+    gates = [pltpu.SemaphoreType.REGULAR((bits - 1,))] if staged else []
 
     hbm = pl.BlockSpec(memory_space=pl.ANY)
     dma = pltpu.SemaphoreType.DMA
@@ -426,16 +464,17 @@
             vmem((slots, main + LANE, items), half),
             vmem((chunks * kchunk, LANE), jnp.float32),
             vmem((nw * rows * SIDE, items), jnp.float32),
-            vmem((chunks, nw, rows, SIDE, items), half),
+            vmem((chunks * nw, rows, SIDE, items), half),
             vmem((chunks, nw, rows, SIDE, items), half),
             vmem((rows, full // LANE, 2 * chunks * kchunk, LANE), half),
             vmem((rows, layers, full), jnp.float32),
             dma((5,)),
-            dma((2, nl - 1, chunks, 2)),
-            dma((2, nl - 1, chunks, 2)),
-            dma((chunks, nw)),
-            dma((chunks, nw)),
-        ],
+            dma((2, nl - 1, 2)),
+            dma((nl - 1, chunks)),
+            dma((nl - 1, tiles)),
+            dma((1,)),
+            dma((chunks,)),
+        ] + gates,
         compiler_params=pltpu.CompilerParams(collective_id=0, has_side_effects=True, vmem_limit_bytes=52 << 20),
     )(place(wave_pair), place(lat_slot), place(spectral), place(leg_t))
 

time: 36.2 us -> 33.9 us (0.936)
  Pallas kernels: 34.8 us -> 32.6 us
    pallas_call x1, Pallas kernels: 34.8 us -> 32.6 us  [on_device(): pl.pallas_call(functools.partial(kernel, nw, nl, slots, wave_count, bound...]
where the time goes in v4:
time: 33.9 us; the launch traced here: 33.8 us
  Pallas kernels  32.6 us (96%)
  local copies, waits for them, and re-layouts  1.19 us (4%)
    pallas_call x1, Pallas kernels, on_device(): pl.pallas_call(functools.partial(kernel, nw, nl, slots, wave_count, bound...  32.6 us
    unnamed x1, local copies, waits for them, and re-layouts  1.19 us

profile of v4, /device:TPU:0, one launch (start us, length us, event | category | flops | bytes accessed | tf_op | source)
XLA Modules:
  0.0 33.8 jit_solution(7103477332203140830)
XLA Ops:
  0.0 32.6 %shard_map.46 = bf16[8,64,1616]{2,1,0:T(8,128)(2,1)S(1)} custom-call(s32[200]{0:T(256)} %wp_hbm.1, s32[64]{0:T(128)} %lat_hbm.1, bf16[25,401,128]{2,1,0:T(8,128)(2,1)} %spec_hbm.1, bf16[25,16,401]{2,1,0:T(8,128)(2,1)} %bitcast.1), custom_call_target="tpu_custom_call" | custom-call | tf_op jit(solution)/shard_map/pallas_call | solution.py:452
  32.6 1.2 %copy.6 = bf16[8,64,1616]{2,1,0:T(8,128)(2,1)} copy(bf16[8,64,1616]{2,1,0:T(8,128)(2,1)S(1)} %shard_map.46) | data formatting | bytes 3309568

commit v5 on v4

--- a/solution.py
+++ b/solution.py
@@ -76,7 +76,7 @@
     nw, nl, slots, wave_count, bounds, groups, per_tile,
     wp_hbm, lat_hbm, spec_hbm, leg_hbm, out_ref,
     wp, lat, spec, own, leg, tail, wts, waves, stage, snd, rcv, basis, part,
-    loc_sem, ag_send, main_recv, tail_recv, aa_send, aa_recv, *gate,
+    loc_sem, ag_send, main_recv, tail_recv, aa_send, aa_recv, gate,
 ):
     wi = lax.axis_index("wav")
     li = lax.axis_index("lev")
@@ -108,26 +108,55 @@
     leg_copy, own_copy, wp_copy, lat_copy, spec_copy = copies
 
     barrier = pltpu.get_barrier_semaphore()
-    for step in (1, -1):
-        @pl.when((li + step >= 0) & (li + step < nl))
+    order = exchange_order(nw)
+    stages = gate.shape[0] - 2
+    first = [k for k in order if near(k)] if stages else order
+    direct = [k for k in first if not k & 1]
+
+    def tell(sem, w, l):
+        pl.semaphore_signal(sem, inc=1, device_id=(w, l), device_id_type=fmt)
+
+    lower = jnp.where(li > 0, 1, 0)
+    higher = 0
+    for k in first:
+        to, source = partner(wi, k, nw, True), partner(wi, k, nw, False)
+        lower += jnp.where(source < wi, 1, 0)
+        higher += jnp.where(to > wi, 1, 0) if nw & (nw - 1) == 0 else jnp.where(source > wi, 1, 0)
+
+    @pl.when(li + 1 < nl)
+    def _():
+        tell(barrier, wi, li + 1)
+
+    for k in first:
+        to = partner(wi, k, nw, True)
+
+        @pl.when(to > wi)
         def _():
-            pl.semaphore_signal(barrier, inc=1, device_id=(wi, li + step), device_id_type=fmt)
-    order = exchange_order(nw)
-    first = [k for k in order if near(k)] if gate else order
+            tell(barrier, to, li)
+
+    @pl.when(lower > 0)
+    def _():
+        pl.semaphore_wait(barrier, lower)
+
+    @pl.when(li > 0)
+    def _():
+        tell(gate.at[1], wi, li - 1)
+
     for k in first:
-        pl.semaphore_signal(barrier, inc=1, device_id=(partner(wi, k, nw, True), li), device_id_type=fmt)
-    beside = jnp.where(li > 0, 1, 0) + jnp.where(li < nl - 1, 1, 0)
-    pl.semaphore_wait(barrier, beside + len(first))
-    direct = [k for k in first if not k & 1]
+        to = partner(wi, k, nw, True)
+
+        @pl.when(to < wi)
+        def _():
+            tell(gate.at[0], to, li)
 
     def relay(stage):
         for k in direct:
-            pl.semaphore_signal(gate[0].at[stage], inc=1, device_id=(partner(wi, k, nw, True), li), device_id_type=fmt)
+            tell(gate.at[2 + stage], partner(wi, k, nw, True), li)
 
     def everyone():
-        for stage in range(len(direct) - 1 if gate else 0):
-            pl.semaphore_wait(gate[0].at[stage], len(direct))
-            if stage + 1 < len(direct) - 1:
+        for stage in range(stages):
+            pl.semaphore_wait(gate.at[2 + stage], len(direct))
+            if stage + 1 < stages:
                 relay(stage + 1)
 
     def fresh(c):
@@ -165,8 +194,8 @@
             return li - 1 - k >= 0, jnp.maximum(li - 1 - k, 0)
         return li + 1 + k < nl, jnp.minimum(li + 1 + k, nl - 1)
 
-    def send(k, c, pieces=(0, 1)):
-        for way in range(2):
+    def send(k, c, pieces=(0, 1), ways=(0, 1)):
+        for way in ways:
             going, block = sends(way, k)
 
             @pl.when(going)
@@ -208,7 +237,7 @@
         )
 
     leg_copy.wait()
-    send(0, 0, (0,))
+    send(0, 0, (0,), (1,))
     own_copy.wait()
     place_t = lax.broadcasted_iota(jnp.int32, (rest, LANE), 0)
     place_x = lax.broadcasted_iota(jnp.int32, (rest, LANE), 1)
@@ -220,12 +249,17 @@
                 place = jnp.where(place_x == place_t + n * rest, 1.0, 0.0).astype(half)
                 total += jnp.dot(own[s, :, main:], place, preferred_element_type=jnp.float32)
         tail[li, t] = total.astype(half)
-    send(0, 0, (1,))
+    send(0, 0, (1,), (1,))
     ahead = min(chunks, 3)
     for c in range(1, ahead):
-        send(0, c)
-    if gate:
-        relay(0)
+        send(0, c, ways=(1,))
+
+    @pl.when(li + 1 < nl)
+    def _():
+        pl.semaphore_wait(gate.at[1], 1)
+
+    for c in range(ahead):
+        send(0, c, ways=(0,))
 
     waves[...] = jnp.full_like(waves, -1.0)
     wp_copy.wait()
@@ -242,6 +276,12 @@
         return carry
 
     lax.fori_loop(0, nw, place_waves, 0)
+    @pl.when(higher > 0)
+    def _():
+        pl.semaphore_wait(gate.at[0], higher)
+
+    if stages:
+        relay(0)
 
     stage[...] = jnp.zeros_like(stage)
     out_i = lax.broadcasted_iota(jnp.int32, (items, items), 1)
@@ -386,7 +426,7 @@
             done["made"] += 1
 
     spec_copy.wait()
-    polls = sorted(((k, c) for k in range(nl - 1) for c in range(chunks)), key=lambda p: (p[0] + p[1], p[0]))
+    polls = sorted(((k, c) for k in range(nl - 1) for c in range(chunks)), key=lambda p: (1.5 * p[0] + p[1], p[0]))
     shown = 0
     for k, c in polls:
         arrive(k, c)
@@ -441,8 +481,7 @@
     kchunk = nw * SIDE
 
     bits = (nw >> 1).bit_length() - 1
-    staged = nw & (nw - 1) == 0 and bits > 1
-    gates = [pltpu.SemaphoreType.REGULAR((bits - 1,))] if staged else []
+    stages = max(0, bits - 1) if nw & (nw - 1) == 0 else 0
 
     hbm = pl.BlockSpec(memory_space=pl.ANY)
     dma = pltpu.SemaphoreType.DMA
@@ -474,7 +513,8 @@
             dma((nl - 1, tiles)),
             dma((1,)),
             dma((chunks,)),
-        ] + gates,
+            pltpu.SemaphoreType.REGULAR((2 + stages,)),
+        ],
         compiler_params=pltpu.CompilerParams(collective_id=0, has_side_effects=True, vmem_limit_bytes=52 << 20),
     )(place(wave_pair), place(lat_slot), place(spectral), place(leg_t))
 

time: 33.9 us -> 33.5 us (0.988)
  Pallas kernels: 32.6 us -> 32.2 us
    pallas_call x1, Pallas kernels: 32.6 us -> 32.2 us  [on_device(): pl.pallas_call(functools.partial(kernel, nw, nl, slots, wave_count, bound...]
where the time goes in v5:
time: 33.5 us; the launch traced here: 33.4 us
  Pallas kernels  32.2 us (96%)
  local copies, waits for them, and re-layouts  1.19 us (4%)
    pallas_call x1, Pallas kernels, on_device(): pl.pallas_call(functools.partial(kernel, nw, nl, slots, wave_count, bound...  32.2 us
    unnamed x1, local copies, waits for them, and re-layouts  1.19 us

profile of v5, /device:TPU:0, one launch (start us, length us, event | category | flops | bytes accessed | tf_op | source)
XLA Modules:
  0.0 33.4 jit_solution(13863155136552316508)
XLA Ops:
  0.0 32.2 %shard_map.46 = bf16[8,64,1616]{2,1,0:T(8,128)(2,1)S(1)} custom-call(s32[200]{0:T(256)} %wp_hbm.1, s32[64]{0:T(128)} %lat_hbm.1, bf16[25,401,128]{2,1,0:T(8,128)(2,1)} %spec_hbm.1, bf16[25,16,401]{2,1,0:T(8,128)(2,1)} %bitcast.1), custom_call_target="tpu_custom_call" | custom-call | tf_op jit(solution)/shard_map/pallas_call | solution.py:491
  32.2 1.2 %copy.6 = bf16[8,64,1616]{2,1,0:T(8,128)(2,1)} copy(bf16[8,64,1616]{2,1,0:T(8,128)(2,1)S(1)} %shard_map.46) | data formatting | bytes 3309568

commit v6 on v5

--- a/solution.py
+++ b/solution.py
@@ -74,20 +74,19 @@
 
 def kernel(
     nw, nl, slots, wave_count, bounds, groups, per_tile,
-    wp_hbm, lat_hbm, spec_hbm, leg_hbm, out_ref,
-    wp, lat, spec, own, leg, tail, wts, waves, stage, snd, rcv, basis, part,
+    wp_hbm, lat_hbm, spec_hbm, leg_hbm, part, late, got,
+    wp, lat, spec, own, leg, tail, wts, waves, stage, snd, rcv, basis,
     loc_sem, ag_send, main_recv, tail_recv, aa_send, aa_recv, gate,
 ):
     wi = lax.axis_index("wav")
     li = lax.axis_index("lev")
     chunks = len(bounds)
-    rows, layers, width = out_ref.shape
+    rows, layers, full = part.shape
     fold = spec.shape[1]
     main = leg.shape[3]
     rest = fold - main
     items = 2 * layers
-    blocks = basis.shape[1]
-    full = blocks * LANE
+    blocks = full // LANE
     kchunk = nw * SIDE
     qtot = nw * rows
     fmt = pl.DeviceIdType.MESH
@@ -167,7 +166,7 @@
         return pltpu.make_async_remote_copy(
             src_ref=view,
             dst_ref=view,
-            send_sem=ag_send.at[way, k, piece],
+            send_sem=ag_send.at[way, piece],
             recv_sem=recv,
             device_id=(wi, li + 1 - 2 * way),
             device_id_type=fmt,
@@ -341,9 +340,14 @@
             c1 = c0 * sc + s0 * ss
             s1 = s0 * sc - c0 * ss
             twice = sc + sc
+            final = c in groups[-1]
+            table = late if final else basis
+            base = group_starts[-1] if final else 0
             for b in range(blocks):
-                basis[r, b, real0 + k0 : real0 + k0 + KB, :] = c0.astype(half)
-                basis[r, b, imag0 + k0 : imag0 + k0 + KB, :] = s0.astype(half)
+                keep = lane + b * LANE < counts[i]
+                cb, sb = (jnp.where(keep, c0, 0.0), jnp.where(keep, s0, 0.0)) if final else (c0, s0)
+                table[r, b, real0 - base + k0 : real0 - base + k0 + KB, :] = cb.astype(half)
+                table[r, b, imag0 - base + k0 : imag0 - base + k0 + KB, :] = sb.astype(half)
                 if b + 1 < blocks:
                     c0, c1 = c1, twice * c1 - c0
                     s0, s1 = s1, twice * s1 - s0
@@ -400,12 +404,9 @@
                 value = jnp.dot(lhs, rhs, preferred_element_type=jnp.float32)
                 if g:
                     value = part[r, :, n0:n1] + value
-                if g + 1 < len(groups):
-                    part[r, :, n0:n1] = value
-                else:
+                if g + 2 == len(groups):
                     value = jnp.where(lanes[:, : n1 - n0] + n0 < count, value, 0.0)
-                    stop = min(width, n1)
-                    out_ref[r, :, n0:stop] = value[:, : stop - n0].astype(half)
+                part[r, :, n0:n1] = value
             return carry
 
         lax.fori_loop(0, rows, body, 0, unroll=True)
@@ -444,21 +445,46 @@
                 shown += 1
         work(done["made"] + 1)
     work(len(units))
-    while shown < len(groups):
+    while shown < len(groups) - 1:
         synthesis(shown)
         shown += 1
-
-    for k in range(nl - 1):
-        for way in range(2):
-            going, block = sends(way, k)
-
-            @pl.when(going)
-            def _():
-                hop(way, k, leg.at[block], 0, main_recv.at[k, 0]).wait_send()
-                hop(way, k, tail.at[block], 1, tail_recv.at[k, 0]).wait_send()
+    for n, c in enumerate(groups[-1]):
+        landed(c)
+        got[n] = rcv[c]
+
+    for place in range(nl):
+        for way, number in ((0, place + 1), (1, nl - place)):
+            if number < nl:
+                @pl.when(li == place)
+                def _():
+                    every = pl.ds(0, number)
+                    hop(way, 0, leg.at[every], 0, main_recv.at[0, 0]).wait_send()
+                    hop(way, 0, tail.at[every], 1, tail_recv.at[0, 0]).wait_send()
 
     sent = snd.at[pl.ds(0, chunks * (nw - 1))]
     exchanged(0, sent, sent).wait_send()
+
+
+def finish(alone, part, late, got, out_hbm, rows_buf, out_sem):
+    rows, layers, width = out_hbm.shape
+    full = part.shape[2]
+    items = got.shape[-1]
+    depth = got.shape[1] * got.shape[3]
+    for r in range(rows):
+        v = jnp.concatenate([got[n, :, r].reshape(depth, items) for n in range(got.shape[0])], axis=0)
+        vt = v.T
+        lhs = jnp.concatenate([vt[:layers], vt[layers:]], axis=1)
+        for n0 in range(0, full, COLS):
+            n1 = min(full, n0 + COLS)
+            rhs = jnp.concatenate([late[r, b] for b in range(n0 // LANE, n1 // LANE)], axis=1)
+            value = jnp.dot(lhs, rhs, preferred_element_type=jnp.float32)
+            if not alone:
+                value = part[r, :, n0:n1] + value
+            stop = min(width, n1)
+            rows_buf[r, :, n0:stop] = value[:, : stop - n0].astype(jnp.bfloat16)
+        pltpu.make_async_copy(rows_buf.at[r], out_hbm.at[r], out_sem.at[r]).start()
+    for r in range(rows):
+        pltpu.make_async_copy(rows_buf.at[r], out_hbm.at[r], out_sem.at[r]).wait()
 
 
 def on_device(spectral, legendre, wave_pair, lat_slot):
@@ -488,11 +514,16 @@
     vmem = pltpu.VMEM
     half = jnp.bfloat16
     place = functools.partial(pltpu.with_memory_space_constraint, memory_space=pltpu.HBM)
-    return pl.pallas_call(
+    last = 2 * kchunk * len(groups[-1])
+    handed = pl.pallas_call(
         functools.partial(kernel, nw, nl, slots, wave_count, bounds, groups, per_tile),
-        out_shape=vmem((rows, layers, width), half),
+        out_shape=[
+            vmem((rows, layers, full), jnp.float32),
+            vmem((rows, full // LANE, last, LANE), half),
+            vmem((len(groups[-1]), nw, rows, SIDE, items), half),
+        ],
         in_specs=[hbm, hbm, hbm, hbm],
-        out_specs=pl.BlockSpec(memory_space=vmem),
+        out_specs=[pl.BlockSpec(memory_space=vmem)] * 3,
         scratch_shapes=[
             pltpu.SMEM(wave_pair.shape, jnp.int32),
             pltpu.SMEM(lat_slot.shape, jnp.int32),
@@ -505,18 +536,25 @@
             vmem((nw * rows * SIDE, items), jnp.float32),
             vmem((chunks * nw, rows, SIDE, items), half),
             vmem((chunks, nw, rows, SIDE, items), half),
-            vmem((rows, full // LANE, 2 * chunks * kchunk, LANE), half),
-            vmem((rows, layers, full), jnp.float32),
+            vmem((rows, full // LANE, 2 * chunks * kchunk - last, LANE), half),
             dma((5,)),
-            dma((2, nl - 1, 2)),
+            dma((2, 2)),
             dma((nl - 1, chunks)),
             dma((nl - 1, tiles)),
             dma((1,)),
             dma((chunks,)),
             pltpu.SemaphoreType.REGULAR((2 + stages,)),
         ],
-        compiler_params=pltpu.CompilerParams(collective_id=0, has_side_effects=True, vmem_limit_bytes=52 << 20),
+        compiler_params=pltpu.CompilerParams(collective_id=0, has_side_effects=True, vmem_limit_bytes=44 << 20),
     )(place(wave_pair), place(lat_slot), place(spectral), place(leg_t))
+    return pl.pallas_call(
+        functools.partial(finish, len(groups) == 1),
+        out_shape=jax.ShapeDtypeStruct((rows, layers, width), half),
+        in_specs=[pl.BlockSpec(memory_space=vmem)] * 3,
+        out_specs=hbm,
+        scratch_shapes=[vmem((rows, layers, width), half), dma((rows,))],
+        compiler_params=pltpu.CompilerParams(vmem_limit_bytes=8 << 20),
+    )(*handed)
 
 
 def solution(mesh):

time: 33.5 us -> 33.2 us (level)
  local copies, waits for them, and re-layouts: 1.19 us -> 0 us
  Pallas kernels: 32.2 us -> 33 us
    pallas_call x0 -> x1, Pallas kernels: none -> 1.6 us  [on_device(): pl.pallas_call(functools.partial(finish, len(groups) == 1), out_shape=jax...]
    unnamed x1 -> x0, local copies, waits for them, and re-layouts: 1.19 us -> none
    pallas_call x1, Pallas kernels: 32.2 us -> 31.4 us  [on_device(): pl.pallas_call(functools.partial(kernel, nw, nl, slots, wave_count, bound...]
where the time goes in v6:
time: 33.2 us; the launch traced here: 33.1 us
  Pallas kernels  33 us (99%)
    pallas_call x1, Pallas kernels, on_device(): pl.pallas_call(functools.partial(kernel, nw, nl, slots, wave_count, bound...  31.4 us
    pallas_call x1, Pallas kernels, on_device(): pl.pallas_call(functools.partial(finish, len(groups) == 1), out_shape=jax...  1.6 us

profile of v6, /device:TPU:0, one launch (start us, length us, event | category | flops | bytes accessed | tf_op | source)
XLA Modules:
  0.0 33.1 jit_solution(7939210819081917873)
XLA Ops:
  0.0 31.4 %shard_map.46 = (f32[8,64,1664]{2,1,0:T(8,128)S(1)}, bf16[8,13,128,128]{3,2,1,0:T(8,128)(2,1)S(1)}, bf16[1,8,8,8,128]{4,3,2,1,0:T(8,128)(2,1)S(1)}) custom-call(s32[200]{0:T(256)} %wp_hbm.1, s32[64]{0:T(128)} %lat_hbm.1, bf16[25,401,128]{2,1,0:T(8,128)(2,1)} %spec_hbm.1, bf16[25,16,401]{2,1,0:T(8,128)(2,1)} %bitcast.1), custom_call_target="tpu_custom_call" | custom-call | tf_op jit(solution)/shard_map/pallas_call | solution.py:518
  31.5 1.6 %shard_map.47 = bf16[8,64,1616]{2,1,0:T(8,128)(2,1)} custom-call(f32[8,64,1664]{2,1,0:T(8,128)S(1)} %get-tuple-element.8.part, bf16[8,13,128,128]{3,2,1,0:T(8,128)(2,1)S(1)} %get-tuple-element.9.late, bf16[1,8,8,8,128]{4,3,2,1,0:T(8,128)(2,1)S(1)} %get-tuple-element.10.got), custom_call_target="tpu_custom_call" | custom-call | tf_op jit(solution)/shard_map/pallas_call | solution.py:550

commit v7 on v6

--- a/solution.py
+++ b/solution.py
@@ -448,9 +448,6 @@
     while shown < len(groups) - 1:
         synthesis(shown)
         shown += 1
-    for n, c in enumerate(groups[-1]):
-        landed(c)
-        got[n] = rcv[c]
 
     for place in range(nl):
         for way, number in ((0, place + 1), (1, nl - place)):
@@ -463,6 +460,10 @@
 
     sent = snd.at[pl.ds(0, chunks * (nw - 1))]
     exchanged(0, sent, sent).wait_send()
+
+    for n, c in enumerate(groups[-1]):
+        landed(c)
+        got[n] = rcv[c]
 
 
 def finish(alone, part, late, got, out_hbm, rows_buf, out_sem):

time: 33.2 us -> 33.2 us (level)
  no operation moved by 1% of the time
where the time goes in v7:
time: 33.2 us; the launch traced here: 33.1 us
  Pallas kernels  33 us (99%)
    pallas_call x1, Pallas kernels, on_device(): pl.pallas_call(functools.partial(kernel, nw, nl, slots, wave_count, bound...  31.4 us
    pallas_call x1, Pallas kernels, on_device(): pl.pallas_call(functools.partial(finish, len(groups) == 1), out_shape=jax...  1.6 us

profile of v7, /device:TPU:0, one launch (start us, length us, event | category | flops | bytes accessed | tf_op | source)
XLA Modules:
  0.0 33.1 jit_solution(7136142717624928267)
XLA Ops:
  0.0 31.4 %shard_map.46 = (f32[8,64,1664]{2,1,0:T(8,128)S(1)}, bf16[8,13,128,128]{3,2,1,0:T(8,128)(2,1)S(1)}, bf16[1,8,8,8,128]{4,3,2,1,0:T(8,128)(2,1)S(1)}) custom-call(s32[200]{0:T(256)} %wp_hbm.1, s32[64]{0:T(128)} %lat_hbm.1, bf16[25,401,128]{2,1,0:T(8,128)(2,1)} %spec_hbm.1, bf16[25,16,401]{2,1,0:T(8,128)(2,1)} %bitcast.1), custom_call_target="tpu_custom_call" | custom-call | tf_op jit(solution)/shard_map/pallas_call | solution.py:519
  31.5 1.6 %shard_map.47 = bf16[8,64,1616]{2,1,0:T(8,128)(2,1)} custom-call(f32[8,64,1664]{2,1,0:T(8,128)S(1)} %get-tuple-element.8.part, bf16[8,13,128,128]{3,2,1,0:T(8,128)(2,1)S(1)} %get-tuple-element.9.late, bf16[1,8,8,8,128]{4,3,2,1,0:T(8,128)(2,1)S(1)} %get-tuple-element.10.got), custom_call_target="tpu_custom_call" | custom-call | tf_op jit(solution)/shard_map/pallas_call | solution.py:551
